TPU v7x, 32 devices: a whole 2x2x4 slice. The times are simulated.
32 devices in a mesh: expert: 4 (over y, core), unit: 8 (over z, x).
Axes of the slice: x: 2, y: 2, z: 4, core: 2. Of those that a mesh axis runs over, the one named last changes fastest.
Arguments:
- a_gate: bfloat16 [4, 14336, 4096], P('expert', 'unit'), may hold values from -0.09375 to 0.09375
- a_up: bfloat16 [4, 14336, 4096], P('expert', 'unit'), may hold values from -0.09375 to 0.09375
- b_gate: bfloat16 [4, 14336, 4096], P('expert', 'unit'), may hold values from -0.09375 to 0.09375
- b_up: bfloat16 [4, 14336, 4096], P('expert', 'unit'), may hold values from -0.09375 to 0.09375
- order: int32 [4, 448], P('expert'), may hold values from 0 to 447, each once within a row
- calib: bfloat16 [128, 4096], P(('expert', 'unit')), may hold values from -6 to 6
Outputs:
- merged_gate: bfloat16 [4, 14336, 4096], P('expert', 'unit')
- merged_up: bfloat16 [4, 14336, 4096], P('expert', 'unit')
- hidden: bfloat16 [4, 14336, 128], P('expert', 'unit')
Inputs may be any that keep to these rules, and one draw needn't show every extreme that they name: Each row of order is a permutation of the 448 block numbers.
All inputs are finite; a program needn't handle non-finite values.
Results may differ from a plain program's by a relative error of at most 0.006.
Values may be sent and summed in bfloat16 or wider, within the bound.
A program may use at most 256 MiB of HBM per device.

v0:
```python
import jax
import jax.numpy as jnp
from jax import lax
from jax.sharding import PartitionSpec as P

BLOCK = 32


def average(first, second):
    return ((first.astype(jnp.float32) + second.astype(jnp.float32)) * 0.5).astype(jnp.bfloat16)


def local(a_gate, a_up, b_gate, b_up, order, calib):
    blocks = order.shape[1]
    total = blocks * BLOCK
    inverse = jnp.zeros((blocks,), jnp.int32).at[order[0]].set(jnp.arange(blocks, dtype=jnp.int32))

    def relocate(columns):
        grouped = columns.reshape(blocks, BLOCK, columns.shape[1])
        return jnp.take(grouped, inverse, axis=0).reshape(total, columns.shape[1])

    gathered = (
        lax.all_to_all(b_gate[0], "unit", split_axis=1, concat_axis=0, tiled=True),
        lax.all_to_all(b_up[0], "unit", split_axis=1, concat_axis=0, tiled=True),
    )
    returned = (
        lax.all_to_all(relocate(gathered[0]), "unit", split_axis=0, concat_axis=1, tiled=True),
        lax.all_to_all(relocate(gathered[1]), "unit", split_axis=0, concat_axis=1, tiled=True),
    )
    merged_gate = average(a_gate[0], returned[0])
    merged_up = average(a_up[0], returned[1])
    dims = (((1,), (1,)), ((), ()))
    piece = lax.all_gather(calib, ("expert", "unit"), axis=0, tiled=True)
    gate_pre = lax.dot_general(merged_gate, piece, dims, preferred_element_type=jnp.float32)
    up_pre = lax.dot_general(merged_up, piece, dims, preferred_element_type=jnp.float32)
    hidden = (jax.nn.silu(gate_pre) * up_pre).astype(jnp.bfloat16)
    return (merged_gate[None], merged_up[None], hidden[None])


def solution(mesh):
    in_specs = (
        P("expert", "unit", None),
        P("expert", "unit", None),
        P("expert", "unit", None),
        P("expert", "unit", None),
        P("expert", None),
        P(("expert", "unit"), None),
    )
    out_specs = (P("expert", "unit", None), P("expert", "unit", None), P("expert", "unit", None))
    return jax.shard_map(local, mesh=mesh, in_specs=in_specs, out_specs=out_specs, check_vma=False)
```

profile of v0, /device:TPU:0, one launch (start us, length us, event | category | flops | bytes accessed | tf_op | source)
XLA Modules:
  0.0 1635.2 jit_solution(6001479759196739935)
XLA Ops:
  7.2 18.6 %copy.22 = bf16[1,1792,4096]{1,2,0:T(8,128)(2,1)} copy(bf16[1,1792,4096]{2,1,0:T(8,128)(2,1)} %param.10) | data formatting | bytes 29360128 | tf_op args[2]
  25.8 7.3 all-to-all-start
  33.1 18.6 %copy.26 = bf16[1,1792,4096]{1,2,0:T(8,128)(2,1)} copy(bf16[1,1792,4096]{2,1,0:T(8,128)(2,1)} %param.11) | data formatting | bytes 29360128 | tf_op args[3]
  51.7 299.4 %all-to-all-done = bf16[1792,8,512]{0,2,1:T(8,128)(2,1)} async-done(((bf16[1792,8,512]{0,2,1:T(8,128)(2,1)}), bf16[1792,8,512]{0,2,1:T(8,128)(2,1)}, u32[]{:S(2)}, u32[]{:S(2)}) %all-to-all-start) | async-done | bytes 14680096 | tf_op jit(solution)/shard_map/all_to_all | solution.py:23
  351.1 0.0 copy-start.2
  351.1 5.7 all-to-all-start.2
  356.8 0.0 copy-done.2
  356.8 2.9 scatter_custom_fusion
  359.8 18.7 %copy.23 = bf16[8,1792,512]{2,1,0:T(8,128)(2,1)} copy(bf16[8,1792,512]{1,2,0:T(8,128)(2,1)} %bitcast.3) | data formatting | bytes 29360128 | tf_op jit(solution)/shard_map/all_to_all | solution.py:23
  378.5 295.4 %all-to-all-done.2 = bf16[1792,8,512]{0,2,1:T(8,128)(2,1)} async-done(((bf16[1792,8,512]{0,2,1:T(8,128)(2,1)}), bf16[1792,8,512]{0,2,1:T(8,128)(2,1)}, u32[]{:S(2)}, u32[]{:S(2)}) %all-to-all-start.2) | async-done | bytes 14680096 | tf_op jit(solution)/shard_map/all_to_all | solution.py:24
  673.8 18.7 %copy.27 = bf16[8,1792,512]{2,1,0:T(8,128)(2,1)} copy(bf16[8,1792,512]{1,2,0:T(8,128)(2,1)} %bitcast.9) | data formatting | bytes 29360128 | tf_op jit(solution)/shard_map/all_to_all | solution.py:24
  692.5 18.6 %gather_fusion = bf16[448,32,512]{2,1,0:T(8,128)(2,1)} fusion(bf16[448,32,512]{2,1,0:T(8,128)(2,1)} %bitcast.50, s32[1024]{0:T(1024)S(1)} %pad_clamp_fusion), kind=kCustom, calls=%fused_computation.clone | custom fusion | bytes 29361920 | tf_op jit(solution)/shard_map/jit(_take)/gather | solution.py:20
  711.1 18.6 %gather_fusion.1 = bf16[448,32,512]{2,1,0:T(8,128)(2,1)} fusion(bf16[448,32,512]{2,1,0:T(8,128)(2,1)} %bitcast.52, s32[1024]{0:T(1024)S(1)} %pad_clamp_fusion), kind=kCustom, calls=%fused_computation.1.clone | custom fusion | bytes 29361920 | tf_op jit(solution)/shard_map/jit(_take)/gather | solution.py:20
  729.7 17.3 %broadcast_select_fusion = (bf16[448,32,512]{2,1,0:T(8,128)(2,1)S(1)}, bf16[448,32,512]{2,1,0:T(8,128)(2,1)}) fusion(bf16[448,32,512]{2,1,0:T(8,128)(2,1)} %gather_fusion.1, pred[448]{0:T(512)(128)(4,1)S(1)} %compare_and_fusion, bf16[448,32,512]{2,1,0:T(8,128)(2,1)} %gather_fusion), kind=kLoop, calls=%fused_computation.19 | loop fusion | flops 14680064 | bytes 58720704 | tf_op jit(solution)/shard_map/jit(_take)/select_n | solution.py:20
  747.0 321.5 %all_to_all.58 = bf16[8,1792,512]{2,1,0:T(8,128)(2,1)} all-to-all(bf16[8,1792,512]{2,1,0:T(8,128)(2,1)S(1)} %bitcast.51), channel_id=1, replica_groups=mesh['expert'=4,'unit'=8] {'unit'}, dimensions={0} | all-to-all | bytes 29360128 | tf_op jit(solution)/shard_map/all_to_all | solution.py:28
  1068.5 5.5 all-to-all-start.1
  1074.0 0.2 all-gather.3.cloned.1.call-start
  1074.2 0.5 all-gather.3.cloned.1.call-update
  1074.7 18.6 %copy.21 = bf16[1,1792,4096]{1,2,0:T(8,128)(2,1)} copy(bf16[1,1792,4096]{2,1,0:T(8,128)(2,1)} %param.8) | data formatting | bytes 29360128 | tf_op args[0]
  1093.4 18.8 %copy.25 = bf16[1,1792,4096]{1,2,0:T(8,128)(2,1)} copy(bf16[1,1792,4096]{2,1,0:T(8,128)(2,1)} %param.9) | data formatting | bytes 29360128 | tf_op args[1]
  1112.1 286.1 %all-gather.3.cloned.1.call-done = bf16[32,4,4096]{2,1,0:T(4,128)(2,1)} async-done(((bf16[1,4,4096]{2,1,0:T(4,128)(2,1)}), bf16[32,4,4096]{2,1,0:T(4,128)(2,1)}) %all-gather.3.cloned.1.call-update) | async-done | bytes 1048592 | tf_op jit(solution)/shard_map/all_gather | solution.py:33
  1398.2 1.3 reshape.132
  1399.5 16.8 %convert_bitcast_fusion.2 = f32[1792,8,512]{2,0,1:T(8,128)} fusion(bf16[8,1792,512]{2,1,0:T(8,128)(2,1)} %all_to_all.58), kind=kLoop, calls=%fused_computation.17 | loop fusion | flops 7340032 | bytes 44040192 | tf_op jit(solution)/shard_map/convert_element_type | solution.py:10
  1416.3 27.6 %copy.28 = f32[1792,8,512]{0,2,1:T(8,128)} copy(f32[1792,8,512]{2,0,1:T(8,128)} %convert_bitcast_fusion.2) | data formatting | bytes 58720256 | tf_op jit(solution)/shard_map/convert_element_type | solution.py:10
  1444.0 0.0 copy-start
  1444.0 20.5 %fusion.9 = bf16[1792,4096]{0,1:T(8,128)(2,1)} fusion(bf16[1,1792,4096]{1,2,0:T(8,128)(2,1)} %copy.25, f32[1792,8,512]{0,2,1:T(8,128)} %copy.28), kind=kLoop, calls=%fused_computation.16 | loop fusion | flops 29360128 | bytes 58720256 | tf_op jit(solution)/shard_map/convert_element_type | solution.py:10
  1464.5 6.9 copy-done
  1471.4 14.6 fusion.6
  1486.0 0.0 all-to-all-done.1
  1486.0 16.8 %convert_bitcast_fusion.3 = f32[1792,8,512]{2,0,1:T(8,128)} fusion(bf16[8,1792,512]{2,1,0:T(8,128)(2,1)} %all-to-all-done.1), kind=kLoop, calls=%fused_computation.18 | loop fusion | flops 7340032 | bytes 44040192 | tf_op jit(solution)/shard_map/convert_element_type | solution.py:10
  1502.8 27.6 %copy.24 = f32[1792,8,512]{0,2,1:T(8,128)} copy(f32[1792,8,512]{2,0,1:T(8,128)} %convert_bitcast_fusion.3) | data formatting | bytes 58720256 | tf_op jit(solution)/shard_map/convert_element_type | solution.py:10
  1530.5 0.0 copy-start.1
  1530.5 20.5 %fusion.4 = bf16[1792,4096]{0,1:T(8,128)(2,1)} fusion(bf16[1,1792,4096]{1,2,0:T(8,128)(2,1)} %copy.21, f32[1792,8,512]{0,2,1:T(8,128)} %copy.24), kind=kLoop, calls=%fused_computation.11 | loop fusion | flops 29360128 | bytes 58720256 | tf_op jit(solution)/shard_map/convert_element_type | solution.py:10
  1551.0 6.9 copy-done.1
  1557.9 14.6 fusion.1
  1572.5 20.1 %copy.32 = bf16[1,1792,4096]{2,1,0:T(8,128)(2,1)} copy(bf16[1,1792,4096]{1,2,0:T(8,128)(2,1)} %fusion.6) | data formatting | bytes 29360128
  1592.6 20.1 %copy.31 = bf16[1,1792,4096]{2,1,0:T(8,128)(2,1)} copy(bf16[1,1792,4096]{1,2,0:T(8,128)(2,1)} %fusion.1) | data formatting | bytes 29360128
  1612.7 7.3 fusion.14
  1620.0 8.3 fusion.11
  (5 shorter events, 0.0 us)
Async XLA Ops:
  25.8 325.3 %all-to-all-start = ((bf16[1792,8,512]{0,2,1:T(8,128)(2,1)}), bf16[1792,8,512]{0,2,1:T(8,128)(2,1)}, u32[]{:S(2)}, u32[]{:S(2)}) async-start(bf16[1792,8,512]{0,2,1:T(8,128)(2,1)} %bitcast.48), calls=%async_computation | async-start | bytes 29360128 | tf_op jit(solution)/shard_map/all_to_all | solution.py:23
  351.1 5.7 copy-start.2
  351.1 322.8 %all-to-all-start.2 = ((bf16[1792,8,512]{0,2,1:T(8,128)(2,1)}), bf16[1792,8,512]{0,2,1:T(8,128)(2,1)}, u32[]{:S(2)}, u32[]{:S(2)}) async-start(bf16[1792,8,512]{0,2,1:T(8,128)(2,1)} %bitcast.47), calls=%async_computation.2 | async-start | bytes 29360128 | tf_op jit(solution)/shard_map/all_to_all | solution.py:24
  1068.5 417.6 %all-to-all-start.1 = ((bf16[8,1792,512]{2,1,0:T(8,128)(2,1)}), bf16[8,1792,512]{2,1,0:T(8,128)(2,1)}, u32[]{:S(2)}, u32[]{:S(2)}) async-start(bf16[8,1792,512]{2,1,0:T(8,128)(2,1)} %bitcast.49), calls=%async_computation.1 | async-start | bytes 29360128 | tf_op jit(solution)/shard_map/all_to_all | solution.py:27
  1074.0 324.2 %all-gather.3.cloned.1.call-start = ((), (), s32[]{:S(2)}) async-start(), calls=%async_computation.4 | async-start | bytes 1081344 | tf_op jit(solution)/shard_map/all_gather | solution.py:33
  1444.0 27.5 %copy-start = (f32[1792,8,512]{0,2,1:T(8,128)S(1)}, f32[1792,8,512]{0,2,1:T(8,128)}, u32[]{:S(2)}) copy-start(f32[1792,8,512]{0,2,1:T(8,128)} %copy.28) | copy-start | bytes 88080384
  1530.5 27.5 %copy-start.1 = (f32[1792,8,512]{0,2,1:T(8,128)S(1)}, f32[1792,8,512]{0,2,1:T(8,128)}, u32[]{:S(2)}) copy-start(f32[1792,8,512]{0,2,1:T(8,128)} %copy.24) | copy-start | bytes 88080384
Sparse Core Ops, SparseCore 0:
  1077.8 320.3 all-gather.2
where the time goes:
time: 1640 us
  waiting for transfers between devices  881 us (54%)
  blocking collectives  322 us (20%)
  local copies, waits for them, and re-layouts  263 us (16%)
  other arithmetic  121 us (7%)
  starting transfers between devices  18.7 us (1%)
    all_to_all x1, blocking collectives, local(): lax.all_to_all(relocate(gathered[1]), 'unit', split_axis=0, concat_axis=1...  322 us
    all_to_all x1, waiting for transfers between devices, local(): lax.all_to_all(b_gate[0], 'unit', split_axis=1, concat_axis=0, tiled=True)  299 us
    all_to_all x1, waiting for transfers between devices, local(): lax.all_to_all(b_up[0], 'unit', split_axis=1, concat_axis=0, tiled=True)  295 us
    all_gather x1, waiting for transfers between devices, local(): piece = lax.all_gather(calib, ('expert', 'unit'), axis=0, tiled=True)  286 us
    unnamed x13, local copies, waits for them, and re-layouts  130 us
    convert_element_type x4, other arithmetic, average(): ((first.astype(jnp.float32) + second.astype(jnp.float32)) * 0.5).astype(j...  70.3 us
    convert_element_type x2, local copies, waits for them, and re-layouts, average(): second.astype(jnp.float32)  55.3 us
    gather x2, local copies, waits for them, and re-layouts, relocate(): return jnp.take(grouped, inverse, axis=0).reshape(total, columns.shape[1])  37.1 us
  transfers between devices with their start and end apart: 4, of which 3 were waited for; matrix products, arithmetic and copies ran while one was open for 10% of the time, Pallas kernels for 0%

commit v1 on v0

--- a/solution.py
+++ b/solution.py
@@ -30,7 +30,8 @@
     merged_gate = average(a_gate[0], returned[0])
     merged_up = average(a_up[0], returned[1])
     dims = (((1,), (1,)), ((), ()))
-    piece = lax.all_gather(calib, ("expert", "unit"), axis=0, tiled=True)
+    sent = jnp.stack([calib] * lax.axis_size(("expert", "unit")))
+    piece = jnp.concatenate(lax.all_to_all(sent, ("expert", "unit"), 0, 0), axis=0)
     gate_pre = lax.dot_general(merged_gate, piece, dims, preferred_element_type=jnp.float32)
     up_pre = lax.dot_general(merged_up, piece, dims, preferred_element_type=jnp.float32)
     hidden = (jax.nn.silu(gate_pre) * up_pre).astype(jnp.bfloat16)

time: 1640 us -> 1500 us (0.915)
  waiting for transfers between devices: 881 us -> 782 us
  other arithmetic: 121 us -> 96.6 us
    all_gather x1 -> x0, waiting for transfers between devices: 286 us -> none  [local(): piece = lax.all_gather(calib, ('expert', 'unit'), axis=0, tiled=True)]
    all_to_all x1 -> x2, waiting for transfers between devices: 0.01 us -> 188 us  [the longest x1 188 us: local(): lax.all_to_all(relocate(gathered[1]), 'unit', split_axis=0, concat_axis=1...]
    convert_element_type x4 -> x2, other arithmetic: 70.3 us -> 40.9 us  [average(): ((first.astype(jnp.float32) + second.astype(jnp.float32)) * 0.5).astype(j...]
    unnamed x13 -> x10, local copies, waits for them, and re-layouts: 130 us -> 115 us
  transfers between devices with their start and end apart: 4 -> 4, of which waited for: 3 -> 3; matrix products, arithmetic and copies ran while one was open for 10% -> 17% of each run, Pallas kernels for 0% -> 0%
where the time goes in v1:
time: 1500 us; the launch traced here: 1490 us
  waiting for transfers between devices  782 us (52%)
  blocking collectives  326 us (22%)
  local copies, waits for them, and re-layouts  249 us (17%)
  other arithmetic  96.6 us (6%)
  starting transfers between devices  22.3 us (1%)
  matrix products  15.6 us (1%)
    all_to_all x1, blocking collectives, local(): lax.all_to_all(relocate(gathered[0]), 'unit', split_axis=0, concat_axis=1...  326 us
    all_to_all x1, waiting for transfers between devices, local(): lax.all_to_all(b_gate[0], 'unit', split_axis=1, concat_axis=0, tiled=True)  299 us
    all_to_all x1, waiting for transfers between devices, local(): lax.all_to_all(b_up[0], 'unit', split_axis=1, concat_axis=0, tiled=True)  295 us
    all_to_all x1, waiting for transfers between devices, local(): lax.all_to_all(relocate(gathered[1]), 'unit', split_axis=0, concat_axis=1...  188 us
    unnamed x10, local copies, waits for them, and re-layouts  115 us
    convert_element_type x2, local copies, waits for them, and re-layouts, average(): second.astype(jnp.float32)  55.3 us
    convert_element_type x2, other arithmetic, average(): ((first.astype(jnp.float32) + second.astype(jnp.float32)) * 0.5).astype(j...  40.9 us
    gather x2, local copies, waits for them, and re-layouts, relocate(): return jnp.take(grouped, inverse, axis=0).reshape(total, columns.shape[1])  37.1 us
  transfers between devices with their start and end apart: 4, of which 3 were waited for; matrix products, arithmetic and copies ran while one was open for 17% of the time, Pallas kernels for 0%

profile of v1, /device:TPU:0, one launch (start us, length us, event | category | flops | bytes accessed | tf_op | source)
XLA Modules:
  0.0 1492.8 jit_solution(2674051864412226067)
XLA Ops:
  0.6 18.6 %copy.10 = bf16[1,1792,4096]{1,2,0:T(8,128)(2,1)} copy(bf16[1,1792,4096]{2,1,0:T(8,128)(2,1)} %param.10) | data formatting | bytes 29360128 | tf_op args[2]
  19.3 7.3 all-to-all-start
  26.5 18.6 %copy.14 = bf16[1,1792,4096]{1,2,0:T(8,128)(2,1)} copy(bf16[1,1792,4096]{2,1,0:T(8,128)(2,1)} %param.11) | data formatting | bytes 29360128 | tf_op args[3]
  45.2 299.4 %all-to-all-done = bf16[1792,8,512]{0,2,1:T(8,128)(2,1)} async-done(((bf16[1792,8,512]{0,2,1:T(8,128)(2,1)}), bf16[1792,8,512]{0,2,1:T(8,128)(2,1)}, u32[]{:S(2)}, u32[]{:S(2)}) %all-to-all-start) | async-done | bytes 14680096 | tf_op jit(solution)/shard_map/all_to_all | solution.py:23
  344.5 0.0 copy-start.1
  344.5 5.7 all-to-all-start.2
  350.2 0.0 copy-done.1
  350.3 2.9 scatter_custom_fusion
  353.2 0.0 copy-start
  353.2 18.7 %copy.11 = bf16[8,1792,512]{2,1,0:T(8,128)(2,1)} copy(bf16[8,1792,512]{1,2,0:T(8,128)(2,1)} %bitcast.3) | data formatting | bytes 29360128 | tf_op jit(solution)/shard_map/all_to_all | solution.py:23
  371.9 295.4 %all-to-all-done.2 = bf16[1792,8,512]{0,2,1:T(8,128)(2,1)} async-done(((bf16[1792,8,512]{0,2,1:T(8,128)(2,1)}), bf16[1792,8,512]{0,2,1:T(8,128)(2,1)}, u32[]{:S(2)}, u32[]{:S(2)}) %all-to-all-start.2) | async-done | bytes 14680096 | tf_op jit(solution)/shard_map/all_to_all | solution.py:24
  667.3 0.0 copy-done
  667.3 1.5 stack.2
  668.8 3.7 all-to-all-start.4
  672.4 18.7 %copy.15 = bf16[8,1792,512]{2,1,0:T(8,128)(2,1)} copy(bf16[8,1792,512]{1,2,0:T(8,128)(2,1)} %bitcast.9) | data formatting | bytes 29360128 | tf_op jit(solution)/shard_map/all_to_all | solution.py:24
  691.2 18.6 %gather_fusion = bf16[448,32,512]{2,1,0:T(8,128)(2,1)} fusion(bf16[448,32,512]{2,1,0:T(8,128)(2,1)} %bitcast.46, s32[1024]{0:T(1024)S(1)} %pad_clamp_fusion), kind=kCustom, calls=%fused_computation.clone | custom fusion | bytes 29361920 | tf_op jit(solution)/shard_map/jit(_take)/gather | solution.py:20
  709.7 18.6 %gather_fusion.1 = bf16[448,32,512]{2,1,0:T(8,128)(2,1)} fusion(bf16[448,32,512]{2,1,0:T(8,128)(2,1)} %bitcast.48, s32[1024]{0:T(1024)S(1)} %pad_clamp_fusion), kind=kCustom, calls=%fused_computation.1.clone | custom fusion | bytes 29361920 | tf_op jit(solution)/shard_map/jit(_take)/gather | solution.py:20
  728.3 22.1 %broadcast_select_fusion = (bf16[448,32,512]{2,1,0:T(8,128)(2,1)}, bf16[448,32,512]{2,1,0:T(8,128)(2,1)}) fusion(bf16[448,32,512]{2,1,0:T(8,128)(2,1)} %gather_fusion.1, pred[448]{0:T(512)(128)(4,1)S(1)} %compare_and_fusion, bf16[448,32,512]{2,1,0:T(8,128)(2,1)} %gather_fusion), kind=kLoop, calls=%fused_computation.15 | loop fusion | flops 14680064 | bytes 58720704 | tf_op jit(solution)/shard_map/jit(_take)/select_n | solution.py:20
  750.4 0.0 all-to-all-done.4
  750.4 325.8 %all_to_all.63 = bf16[8,1792,512]{2,1,0:T(8,128)(2,1)} all-to-all(bf16[8,1792,512]{2,1,0:T(8,128)(2,1)} %bitcast.47), channel_id=1, replica_groups=mesh['expert'=4,'unit'=8] {'unit'}, dimensions={0} | all-to-all | bytes 29360128 | tf_op jit(solution)/shard_map/all_to_all | solution.py:27
  1076.2 5.7 all-to-all-start.3
  1082.0 18.6 %copy.9 = bf16[1,1792,4096]{1,2,0:T(8,128)(2,1)} copy(bf16[1,1792,4096]{2,1,0:T(8,128)(2,1)} %param.8) | data formatting | bytes 29360128 | tf_op args[0]
  1100.6 18.8 %copy.13 = bf16[1,1792,4096]{1,2,0:T(8,128)(2,1)} copy(bf16[1,1792,4096]{2,1,0:T(8,128)(2,1)} %param.9) | data formatting | bytes 29360128 | tf_op args[1]
  1119.4 0.3 reshape.100
  1119.6 16.8 %convert_bitcast_fusion.1 = f32[1792,8,512]{2,0,1:T(8,128)} fusion(bf16[8,1792,512]{2,1,0:T(8,128)(2,1)} %all_to_all.63), kind=kLoop, calls=%fused_computation.10 | loop fusion | flops 7340032 | bytes 44040192 | tf_op jit(solution)/shard_map/convert_element_type | solution.py:10
  1136.4 27.7 %copy.12 = f32[1792,8,512]{0,2,1:T(8,128)} copy(f32[1792,8,512]{2,0,1:T(8,128)} %convert_bitcast_fusion.1) | data formatting | bytes 58720256 | tf_op jit(solution)/shard_map/convert_element_type | solution.py:10
  1164.1 20.4 %fusion.3 = bf16[1,1792,4096]{1,2,0:T(8,128)(2,1)} fusion(f32[1792,8,512]{0,2,1:T(8,128)} %copy.12, bf16[1,1792,4096]{1,2,0:T(8,128)(2,1)} %copy.9), kind=kLoop, calls=%fused_computation.8 | loop fusion | flops 29360128 | bytes 58720256 | tf_op jit(solution)/shard_map/convert_element_type | solution.py:10
  1184.5 20.1 %copy.17 = bf16[1,1792,4096]{2,1,0:T(8,128)(2,1)} copy(bf16[1,1792,4096]{1,2,0:T(8,128)(2,1)} %fusion.3) | data formatting | bytes 29360128
  1204.6 7.3 fusion.6
  1211.9 187.6 %all-to-all-done.3 = bf16[8,1792,512]{2,1,0:T(8,128)(2,1)} async-done(((bf16[8,1792,512]{2,1,0:T(8,128)(2,1)}), bf16[8,1792,512]{2,1,0:T(8,128)(2,1)}, u32[]{:S(2)}, u32[]{:S(2)}) %all-to-all-start.3) | async-done | bytes 14680096 | tf_op jit(solution)/shard_map/all_to_all | solution.py:28
  1399.5 16.8 %convert_bitcast_fusion = f32[1792,8,512]{2,0,1:T(8,128)} fusion(bf16[8,1792,512]{2,1,0:T(8,128)(2,1)} %all-to-all-done.3), kind=kLoop, calls=%fused_computation.9 | loop fusion | flops 7340032 | bytes 44040192 | tf_op jit(solution)/shard_map/convert_element_type | solution.py:10
  1416.3 27.7 %copy.16 = f32[1792,8,512]{0,2,1:T(8,128)} copy(f32[1792,8,512]{2,0,1:T(8,128)} %convert_bitcast_fusion) | data formatting | bytes 58720256 | tf_op jit(solution)/shard_map/convert_element_type | solution.py:10
  1444.0 20.5 %fusion.1 = bf16[1,1792,4096]{1,2,0:T(8,128)(2,1)} fusion(f32[1792,8,512]{0,2,1:T(8,128)} %copy.16, bf16[1,1792,4096]{1,2,0:T(8,128)(2,1)} %copy.13), kind=kLoop, calls=%fused_computation.5 | loop fusion | flops 29360128 | bytes 58720256 | tf_op jit(solution)/shard_map/convert_element_type | solution.py:10
  1464.4 20.1 %copy.18 = bf16[1,1792,4096]{2,1,0:T(8,128)(2,1)} copy(bf16[1,1792,4096]{1,2,0:T(8,128)(2,1)} %fusion.1) | data formatting | bytes 29360128
  1484.5 8.3 fusion.14
  (5 shorter events, 0.0 us)
Async XLA Ops:
  19.3 325.3 %all-to-all-start = ((bf16[1792,8,512]{0,2,1:T(8,128)(2,1)}), bf16[1792,8,512]{0,2,1:T(8,128)(2,1)}, u32[]{:S(2)}, u32[]{:S(2)}) async-start(bf16[1792,8,512]{0,2,1:T(8,128)(2,1)} %bitcast.44), calls=%async_computation | async-start | bytes 29360128 | tf_op jit(solution)/shard_map/all_to_all | solution.py:23
  344.5 5.7 copy-start.1
  344.5 322.8 %all-to-all-start.2 = ((bf16[1792,8,512]{0,2,1:T(8,128)(2,1)}), bf16[1792,8,512]{0,2,1:T(8,128)(2,1)}, u32[]{:S(2)}, u32[]{:S(2)}) async-start(bf16[1792,8,512]{0,2,1:T(8,128)(2,1)} %bitcast.43), calls=%async_computation.2 | async-start | bytes 29360128 | tf_op jit(solution)/shard_map/all_to_all | solution.py:24
  353.2 314.1 %copy-start = (bf16[4,4096]{1,0:T(4,128)(2,1)S(1)}, bf16[4,4096]{1,0:T(4,128)(2,1)}, u32[]{:S(2)}) copy-start(bf16[4,4096]{1,0:T(4,128)(2,1)} %param.13) | copy-start | bytes 98308
  668.8 81.7 %all-to-all-start.4 = ((bf16[32,4,4096]{2,1,0:T(4,128)(2,1)}), bf16[32,4,4096]{2,1,0:T(4,128)(2,1)S(1)}, u32[]{:S(2)}, u32[]{:S(2)}) async-start(bf16[32,4,4096]{2,1,0:T(4,128)(2,1)} %stack.2), calls=%async_computation.4 | async-start | bytes 2097152 | tf_op jit(solution)/shard_map/all_to_all | solution.py:34
  1076.2 323.3 %all-to-all-start.3 = ((bf16[8,1792,512]{2,1,0:T(8,128)(2,1)}), bf16[8,1792,512]{2,1,0:T(8,128)(2,1)}, u32[]{:S(2)}, u32[]{:S(2)}) async-start(bf16[8,1792,512]{2,1,0:T(8,128)(2,1)} %bitcast.45), calls=%async_computation.3 | async-start | bytes 29360128 | tf_op jit(solution)/shard_map/all_to_all | solution.py:28
